TPU v7x, 128 devices: a whole 4x4x4 slice. The times are simulated.
128 devices in a mesh: row: 8 (over x, core), col: 16 (over z, y).
Axes of the slice: x: 4, y: 4, z: 4, core: 2. Of those that a mesh axis runs over, the one named last changes fastest.
Arguments:
- basis: bfloat16 [1152, 256, 128], P(('row', 'col')), may hold values from -1.5 to 1.5
- row_index: int32 [1152, 128], P(('row', 'col')), may hold values from 0 to 255
- group_slot: int32 [1152], P(('row', 'col')), may hold values from 0 to 1535, as said below
- x_blocks: bfloat16 [96, 256, 256], P('row', 'col')
- zinv_blocks: bfloat16 [96, 256, 256], P('row', 'col')
Outputs:
- schur_tiles: float32 [96, 2048, 2048], P('row', None, 'col')
Inputs may be any that keep to these rules, and one draw needn't show every extreme that they name: Values are distinct; group_slot // 16 is the group's PSD block and group_slot % 16 its position there. A group stored on the device at (row index a, col index c) has its position among c * 1 to c + 1 - 1. Of the groups of one device, at most 2 belong to blocks of one index of row (blocks b with b // 12 equal to it), and every device reaches 2 for some index. The positions that the blocks of one index of row have on one index of col hold exactly 9 groups.
All inputs are finite; a program needn't handle non-finite values.
Results may differ from a plain program's by a relative error of at most 0.00048.
Values may be sent and summed in bfloat16 or wider, within the bound.
A program may use at most 192 MiB of HBM per device.

v0:
```python
import jax
import jax.numpy as jnp
from jax import lax
from jax.sharding import PartitionSpec as P

GMAX = 16


def sent_together(arrays, axis, split_dim, concat_dim, along):
    columns = [a.reshape(*a.shape[:along], -1) for a in arrays]
    both = jnp.concatenate(columns, axis=along)
    result, at, done = (
        lax.all_to_all(both, axis, split_axis=split_dim, concat_axis=concat_dim, tiled=True),
        0,
        [],
    )
    for a, column in zip(arrays, columns):
        slab = result[..., at : at + column.shape[along]]
        done.append(slab.reshape(*slab.shape[:along], *a.shape[along:]))
        at += column.shape[along]
    return tuple(done)


def side_by_side(arrays, axis, dim, along):
    widths = [a.shape[along] for a in arrays]
    both = jnp.concatenate(arrays, axis=along)
    result = lax.all_gather(both, axis, axis=dim, tiled=True)
    return tuple(jnp.split(result, [sum(widths[:k]) for k in range(1, len(widths))], axis=along))


def place_rows(selector, values):
    flat_values = values.reshape(values.shape[0], -1)
    moved_rows = jnp.dot(selector, flat_values, preferred_element_type=jnp.float32)
    return moved_rows.astype(values.dtype).reshape((selector.shape[0],) + values.shape[1:])


def place_ints(selector, values):
    moved_rows = jnp.dot(selector, values, preferred_element_type=jnp.int32)
    return moved_rows


def pair_tiles(members):
    stacked, x_full, z_full, rows_all, mask_all, near_basis, near_rows, near_mask = members
    group_width = near_basis.shape[-1]
    order = x_full.shape[0]
    positions = rows_all.shape[0]
    order_ids = jnp.arange(order, dtype=jnp.int32)
    row_pick = (rows_all.reshape(-1)[:, None] == order_ids[None, :]).astype(jnp.bfloat16)
    x_rows = (
        jnp.dot(row_pick, x_full, preferred_element_type=jnp.float32)
        .astype(jnp.bfloat16)
        .reshape(positions, group_width, order)
    )
    z_rows = (
        jnp.dot(row_pick, z_full, preferred_element_type=jnp.float32)
        .astype(jnp.bfloat16)
        .reshape(positions, group_width, order)
    )
    images = jnp.concatenate([stacked[:, 0], x_rows, stacked[:, 1], z_rows], axis=1)
    products = jnp.einsum("pcn,snk->pcsk", images, near_basis, preferred_element_type=jnp.float32)
    products = products.reshape(products.shape[0], products.shape[1], -1)
    column_pick = (order_ids[:, None] == near_rows.reshape(-1)[None, :]).astype(jnp.bfloat16)
    picked = jnp.einsum("pcn,nk->pck", images, column_pick, preferred_element_type=jnp.float32)
    upper = 2 * group_width
    third = 3 * group_width
    tile_sum = (
        products[:, group_width:upper] * picked[:, upper:third]
        + picked[:, group_width:upper] * products[:, upper:third]
    )
    tile_sum = (
        tile_sum
        + products[:, :group_width] * picked[:, third:]
        + picked[:, :group_width] * products[:, third:]
    )
    row_mask = mask_all.astype(jnp.float32)
    column_mask = jnp.repeat(near_mask.astype(jnp.float32), group_width)
    tile_sum = tile_sum * row_mask[:, None, None] * column_mask[None, None, :]
    return tile_sum.reshape(-1, tile_sum.shape[2])


def body(basis, row_index, group_slot, x_blocks, zinv_blocks):
    row_count = lax.axis_size("row")
    col_count = lax.axis_size("col")
    my_row = lax.axis_index("row")
    my_col = lax.axis_index("col")
    groups = basis.shape[0]
    owned = x_blocks.shape[0]
    places = GMAX // col_count
    capacity = (groups + row_count - 1) // row_count
    slot_count = row_count * capacity
    block_of = group_slot // GMAX
    owner_of = block_of // owned
    same_owner = (owner_of[:, None] == owner_of[None, :]).astype(jnp.int32)
    earlier = jnp.sum(jnp.tril(same_owner, -1), axis=1)
    target = owner_of * capacity + earlier
    choose = target[None, :] == jnp.arange(slot_count, dtype=jnp.int32)[:, None]
    send_basis = place_rows(choose.astype(jnp.bfloat16), basis)
    send_rows = place_ints(choose.astype(jnp.int32), row_index)
    send_slot = place_ints(choose.astype(jnp.int32), (group_slot + 1)[:, None])[:, 0] - 1
    got_basis, got_rows, got_slot = (
        lax.all_to_all(send_basis, "row", split_axis=0, concat_axis=0, tiled=True),
        *sent_together((send_rows, send_slot), "row", 0, 0, 1),
    )
    is_valid = got_slot >= 0
    spot_index = (got_slot // GMAX - my_row * owned) * places + (got_slot % GMAX - my_col * places)
    settle = (
        spot_index[None, :] == jnp.arange(owned * places, dtype=jnp.int32)[:, None]
    ) & is_valid[None, :]
    near_basis = place_rows(settle.astype(jnp.bfloat16), got_basis)
    near_basis = near_basis.reshape((owned, places) + near_basis.shape[1:])
    near_rows = place_ints(settle.astype(jnp.int32), got_rows).reshape(owned, places, -1)
    near_mask = (
        jnp.sum(settle.astype(jnp.float32), axis=1).astype(jnp.bfloat16).reshape(owned, places)
    )
    x_full, z_full, all_basis, rows_all, mask_all = (
        *side_by_side((x_blocks, zinv_blocks), "col", 1, 0),
        lax.all_gather(near_basis, "col", axis=1, tiled=True),
        lax.all_gather(near_rows, "col", axis=1, tiled=True),
        lax.all_gather(near_mask, "col", axis=1, tiled=True),
    )
    all_x = jnp.einsum(
        "jpnc,jnm->jpcm", all_basis, x_full, preferred_element_type=jnp.float32
    ).astype(jnp.bfloat16)
    all_z = jnp.einsum(
        "jpnc,jnm->jpcm", all_basis, z_full, preferred_element_type=jnp.float32
    ).astype(jnp.bfloat16)
    stacked = jnp.stack([all_x, all_z], axis=2)
    tile_blocks = lax.map(
        pair_tiles, (stacked, x_full, z_full, rows_all, mask_all, near_basis, near_rows, near_mask)
    )
    return tile_blocks


def solution(mesh):
    placed = (
        P(("row", "col"), None, None),
        P(("row", "col"), None),
        P(("row", "col")),
        P("row", "col", None),
        P("row", "col", None),
    )
    return jax.shard_map(
        body, mesh=mesh, in_specs=placed, out_specs=P("row", None, "col"), check_vma=False
    )
```

profile of v0, /device:TPU:1, one launch (start us, length us, event | category | flops | bytes accessed | tf_op | source)
XLA Modules:
  0.0 411.3 jit_solution(17968727844061814337)
XLA Ops:
  10.7 5.8 %all-to-all-start = ((s32[8,2,129]{2,1,0:T(2,128)}), s32[8,2,129]{2,1,0:T(2,128)S(1)}, u32[]{:S(2)}, u32[]{:S(2)}) async-start(s32[8,2,129]{2,1,0:T(2,128)} %pad_add_fusion), calls=%async_computation | async-start | bytes 32768 | tf_op jit(solution)/shard_map/all_to_all | solution.py:13
  21.2 4.2 %all-to-all-start.1 = ((bf16[16,256,128]{2,1,0:T(8,128)(2,1)}), bf16[16,256,128]{2,1,0:T(8,128)(2,1)S(1)}, u32[]{:S(2)}, u32[]{:S(2)}) async-start(bf16[16,256,128]{2,1,0:T(8,128)(2,1)} %bitcast.45), calls=%async_computation.1 | async-start | bytes 2097152 | tf_op jit(solution)/shard_map/all_to_all | solution.py:101
  25.5 14.8 %all-to-all-done.1 = bf16[16,256,128]{2,1,0:T(8,128)(2,1)S(1)} async-done(((bf16[16,256,128]{2,1,0:T(8,128)(2,1)}), bf16[16,256,128]{2,1,0:T(8,128)(2,1)S(1)}, u32[]{:S(2)}, u32[]{:S(2)}) %all-to-all-start.1) | async-done | bytes 1048608 | tf_op jit(solution)/shard_map/all_to_all | solution.py:101
  43.9 21.8 %all-gather = s32[12,2048]{1,0:T(8,128)S(1)} all-gather(s32[12,128]{1,0:T(8,128)S(1)} %fusion.32), channel_id=2, replica_groups=mesh['row'=8,'col'=16] {'col'}, dimensions={1}, use_global_device_ids=true | all-gather | bytes 104448 | tf_op jit(solution)/shard_map/all_gather | solution.py:118
  65.9 16.1 %all-gather.1 = bf16[16,1,12]{2,1,0:T(2,128)(2,1)S(1)} all-gather(bf16[1,1,12]{2,1,0:T(2,128)(2,1)S(1)} %bitcast.137), channel_id=1, replica_groups=mesh['row'=8,'col'=16] {'col'}, dimensions={0}, use_global_device_ids=true | all-gather | bytes 408 | tf_op jit(solution)/shard_map/all_gather | solution.py:119
  85.4 71.0 %all-gather.5.cloned.1.call-done = bf16[12,16,256,128]{2,3,1,0:T(8,128)(2,1)} async-done(((bf16[12,1,256,128]{2,3,1,0:T(8,128)(2,1)}), bf16[12,16,256,128]{2,3,1,0:T(8,128)(2,1)}) %all-gather.5.cloned.1.call-update) | async-done | bytes 12582928 | tf_op jit(solution)/shard_map/all_gather | solution.py:117
  156.4 11.4 %convert_bitcast_fusion = bf16[12,16,1,128,256]{4,3,1,0,2:T(8,128)(2,1)} fusion(bf16[12,16,256,128]{2,3,1,0:T(8,128)(2,1)} %all-gather.5.cloned.1.call-done, bf16[24,256,256]{2,1,0:T(8,128)(2,1)} %all-gather.7.cloned.1.call-done), kind=kOutput, calls=%fused_computation.45 | convolution fusion | flops 3227516928 | bytes 26738688 | tf_op jit(solution)/shard_map/jpnc,jnm->jpcm/dot_general | solution.py:124
  169.4 7.7 %convert_bitcast_fusion.1 = bf16[12,16,1,128,256]{4,3,1,0,2:T(8,128)(2,1)} fusion(bf16[12,16,256,128]{2,3,1,0:T(8,128)(2,1)S(1)} %copy-done.2, bf16[24,256,256]{2,1,0:T(8,128)(2,1)} %all-gather.7.cloned.1.call-done), kind=kOutput, calls=%fused_computation.46 | convolution fusion | flops 3227516928 | bytes 26738688 | tf_op jit(solution)/shard_map/jpnc,jnm->jpcm/dot_general | solution.py:121
  177.1 20.5 %pad_maximum_fusion.3 = bf16[12,16,2,128,256]{4,3,1,0,2:T(8,128)(2,1)} fusion(bf16[12,16,1,128,256]{4,3,1,0,2:T(8,128)(2,1)} %convert_bitcast_fusion, bf16[12,16,1,128,256]{4,3,1,0,2:T(8,128)(2,1)} %convert_bitcast_fusion.1), kind=kLoop, calls=%fused_computation.44 | loop fusion | flops 12582912 | bytes 50331648 | tf_op jit(solution)/shard_map/stack | solution.py:127
  197.7 206.1 %while.10 = (s32[]{:T(128)}, f32[12,2048,128]{2,1,0:T(8,128)}, bf16[12,16,2,128,256]{4,3,1,0,2:T(8,128)(2,1)}, s32[12,16,128]{2,1,0:T(8,128)S(1)}, bf16[12,256,2...) while((s32[]{:T(128)}, f32[12,2048,128]{2,1,0:T(8,128)}, ...), condition=%wide.region_3.4_spmd, body=%wide.region_2.3_spmd.sunk | while | flops 1648656384 | bytes 39161136 | solution.py:128
  204.7 3.6 fusion.70
  209.4 4.4 %fusion.74 = f32[16,128,128]{2,1,0:T(8,128)S(1)} fusion(f32[16,512,128]{2,1,0:T(8,128)} %fusion.70, f32[16,512,128]{2,1,0:T(8,128)} %fusion.72, f32[]{:T(128)S(6)} %convert.11, f32[16]{0:T(128)S(1)} %fusion.73), kind=kLoop, calls=%fused_computation.8.clone.1 | loop fusion | flops 2359296 | bytes 9437252 | tf_op jit(solution)/shard_map/while/body/eval_jaxpr/mul | solution.py:77
  221.9 3.6 fusion.70
  226.6 4.4 %fusion.74 = f32[16,128,128]{2,1,0:T(8,128)S(1)} fusion(f32[16,512,128]{2,1,0:T(8,128)} %fusion.70, f32[16,512,128]{2,1,0:T(8,128)} %fusion.72, f32[]{:T(128)S(6)} %convert.11, f32[16]{0:T(128)S(1)} %fusion.73), kind=kLoop, calls=%fused_computation.8.clone.1 | loop fusion | flops 2359296 | bytes 9437252 | tf_op jit(solution)/shard_map/while/body/eval_jaxpr/mul | solution.py:77
  239.1 3.6 fusion.70
  243.8 4.4 %fusion.74 = f32[16,128,128]{2,1,0:T(8,128)S(1)} fusion(f32[16,512,128]{2,1,0:T(8,128)} %fusion.70, f32[16,512,128]{2,1,0:T(8,128)} %fusion.72, f32[]{:T(128)S(6)} %convert.11, f32[16]{0:T(128)S(1)} %fusion.73), kind=kLoop, calls=%fused_computation.8.clone.1 | loop fusion | flops 2359296 | bytes 9437252 | tf_op jit(solution)/shard_map/while/body/eval_jaxpr/mul | solution.py:77
  256.2 3.6 fusion.70
  261.0 4.4 %fusion.74 = f32[16,128,128]{2,1,0:T(8,128)S(1)} fusion(f32[16,512,128]{2,1,0:T(8,128)} %fusion.70, f32[16,512,128]{2,1,0:T(8,128)} %fusion.72, f32[]{:T(128)S(6)} %convert.11, f32[16]{0:T(128)S(1)} %fusion.73), kind=kLoop, calls=%fused_computation.8.clone.1 | loop fusion | flops 2359296 | bytes 9437252 | tf_op jit(solution)/shard_map/while/body/eval_jaxpr/mul | solution.py:77
  273.4 3.6 fusion.70
  278.1 4.4 %fusion.74 = f32[16,128,128]{2,1,0:T(8,128)S(1)} fusion(f32[16,512,128]{2,1,0:T(8,128)} %fusion.70, f32[16,512,128]{2,1,0:T(8,128)} %fusion.72, f32[]{:T(128)S(6)} %convert.11, f32[16]{0:T(128)S(1)} %fusion.73), kind=kLoop, calls=%fused_computation.8.clone.1 | loop fusion | flops 2359296 | bytes 9437252 | tf_op jit(solution)/shard_map/while/body/eval_jaxpr/mul | solution.py:77
  290.6 3.6 fusion.70
  295.3 4.4 %fusion.74 = f32[16,128,128]{2,1,0:T(8,128)S(1)} fusion(f32[16,512,128]{2,1,0:T(8,128)} %fusion.70, f32[16,512,128]{2,1,0:T(8,128)} %fusion.72, f32[]{:T(128)S(6)} %convert.11, f32[16]{0:T(128)S(1)} %fusion.73), kind=kLoop, calls=%fused_computation.8.clone.1 | loop fusion | flops 2359296 | bytes 9437252 | tf_op jit(solution)/shard_map/while/body/eval_jaxpr/mul | solution.py:77
  307.8 3.6 fusion.70
  312.5 4.4 %fusion.74 = f32[16,128,128]{2,1,0:T(8,128)S(1)} fusion(f32[16,512,128]{2,1,0:T(8,128)} %fusion.70, f32[16,512,128]{2,1,0:T(8,128)} %fusion.72, f32[]{:T(128)S(6)} %convert.11, f32[16]{0:T(128)S(1)} %fusion.73), kind=kLoop, calls=%fused_computation.8.clone.1 | loop fusion | flops 2359296 | bytes 9437252 | tf_op jit(solution)/shard_map/while/body/eval_jaxpr/mul | solution.py:77
  325.0 3.6 fusion.70
  329.7 4.4 %fusion.74 = f32[16,128,128]{2,1,0:T(8,128)S(1)} fusion(f32[16,512,128]{2,1,0:T(8,128)} %fusion.70, f32[16,512,128]{2,1,0:T(8,128)} %fusion.72, f32[]{:T(128)S(6)} %convert.11, f32[16]{0:T(128)S(1)} %fusion.73), kind=kLoop, calls=%fused_computation.8.clone.1 | loop fusion | flops 2359296 | bytes 9437252 | tf_op jit(solution)/shard_map/while/body/eval_jaxpr/mul | solution.py:77
  342.1 3.6 fusion.70
  346.9 4.4 %fusion.74 = f32[16,128,128]{2,1,0:T(8,128)S(1)} fusion(f32[16,512,128]{2,1,0:T(8,128)} %fusion.70, f32[16,512,128]{2,1,0:T(8,128)} %fusion.72, f32[]{:T(128)S(6)} %convert.11, f32[16]{0:T(128)S(1)} %fusion.73), kind=kLoop, calls=%fused_computation.8.clone.1 | loop fusion | flops 2359296 | bytes 9437252 | tf_op jit(solution)/shard_map/while/body/eval_jaxpr/mul | solution.py:77
  364.0 4.4 %fusion.74 = f32[16,128,128]{2,1,0:T(8,128)S(1)} fusion(f32[16,512,128]{2,1,0:T(8,128)} %fusion.70, f32[16,512,128]{2,1,0:T(8,128)} %fusion.72, f32[]{:T(128)S(6)} %convert.11, f32[16]{0:T(128)S(1)} %fusion.73), kind=kLoop, calls=%fused_computation.8.clone.1 | loop fusion | flops 2359296 | bytes 9437252 | tf_op jit(solution)/shard_map/while/body/eval_jaxpr/mul | solution.py:77
  376.5 3.6 fusion.70
  381.2 4.4 %fusion.74 = f32[16,128,128]{2,1,0:T(8,128)S(1)} fusion(f32[16,512,128]{2,1,0:T(8,128)} %fusion.70, f32[16,512,128]{2,1,0:T(8,128)} %fusion.72, f32[]{:T(128)S(6)} %convert.11, f32[16]{0:T(128)S(1)} %fusion.73), kind=kLoop, calls=%fused_computation.8.clone.1 | loop fusion | flops 2359296 | bytes 9437252 | tf_op jit(solution)/shard_map/while/body/eval_jaxpr/mul | solution.py:77
  398.4 4.4 %fusion.74 = f32[16,128,128]{2,1,0:T(8,128)S(1)} fusion(f32[16,512,128]{2,1,0:T(8,128)} %fusion.70, f32[16,512,128]{2,1,0:T(8,128)} %fusion.72, f32[]{:T(128)S(6)} %convert.11, f32[16]{0:T(128)S(1)} %fusion.73), kind=kLoop, calls=%fused_computation.8.clone.1 | loop fusion | flops 2359296 | bytes 9437252 | tf_op jit(solution)/shard_map/while/body/eval_jaxpr/mul | solution.py:77
  (161 shorter events, 129.1 us)
Async XLA Ops:
  6.5 3.4 copy-start
  6.5 75.5 %all-gather.7.cloned.1.call-start = ((), (), s32[]{:S(2)}) async-start(), calls=%async_computation.3 | async-start | bytes 3342336 | tf_op jit(solution)/shard_map/all_gather | solution.py:27
  10.7 10.4 %all-to-all-start = ((s32[8,2,129]{2,1,0:T(2,128)}), s32[8,2,129]{2,1,0:T(2,128)S(1)}, u32[]{:S(2)}, u32[]{:S(2)}) async-start(s32[8,2,129]{2,1,0:T(2,128)} %pad_add_fusion), calls=%async_computation | async-start | bytes 32768 | tf_op jit(solution)/shard_map/all_to_all | solution.py:13
  21.2 19.2 %all-to-all-start.1 = ((bf16[16,256,128]{2,1,0:T(8,128)(2,1)}), bf16[16,256,128]{2,1,0:T(8,128)(2,1)S(1)}, u32[]{:S(2)}, u32[]{:S(2)}) async-start(bf16[16,256,128]{2,1,0:T(8,128)(2,1)} %bitcast.45), calls=%async_computation.1 | async-start | bytes 2097152 | tf_op jit(solution)/shard_map/all_to_all | solution.py:101
  25.3 131.0 %all-gather.5.cloned.1.call-start = ((), (), s32[]{:S(2)}) async-start(), calls=%async_computation.2 | async-start | bytes 13369344 | tf_op jit(solution)/shard_map/all_gather | solution.py:117
  156.4 13.0 %copy-start.2 = (bf16[12,16,256,128]{2,3,1,0:T(8,128)(2,1)S(1)}, bf16[12,16,256,128]{2,3,1,0:T(8,128)(2,1)}, u32[]{:S(2)}) copy-start(bf16[12,16,256,128]{2,3,1,0:T(8,128)(2,1)} %all-gather.5.cloned.1.call-done) | copy-start | bytes 37748740
  403.8 0.7 copy-start.1
Sparse Core Ops, SparseCore 0:
  9.4 54.1 all-gather.6
  65.8 90.5 all-gather.4
where the time goes:
time: 413 us; the launch traced here: 411 us
  matrix products  126 us (31%)
  waiting for transfers between devices  87.1 us (21%)
  other arithmetic  76.2 us (18%)
  local copies, waits for them, and re-layouts  53.5 us (13%)
  blocking collectives  37.9 us (9%)
  between operations  13.5 us (3%)
  starting transfers between devices  9.97 us (2%)
  loops' own time  7.33 us (2%)
    all_gather x1, waiting for transfers between devices, body(): lax.all_gather(near_basis, 'col', axis=1, tiled=True)  71 us
    mul x12, other arithmetic, pair_tiles(): tile_sum = tile_sum * row_mask[:, None, None] * column_mask[None, None, :]  52.3 us
    dot_general x12, matrix products, pair_tiles(): jnp.einsum('pcn,snk->pcsk', images, near_basis, preferred_element_type=jn...  43 us
    dot_general x12, matrix products, pair_tiles(): jnp.einsum('pcn,nk->pck', images, column_pick, preferred_element_type=jnp...  32.7 us
    all_gather x1, blocking collectives, body(): lax.all_gather(near_rows, 'col', axis=1, tiled=True)  21.8 us
    squeeze x12, local copies, waits for them, and re-layouts, body(): lax.map(pair_tiles, (stacked, x_full, z_full, rows_all, mask_all, near_ba...  20.8 us
    another operation x1, other arithmetic, body(): stacked = jnp.stack([all_x, all_z], axis=2)  20.5 us
    dot_general x12, matrix products, pair_tiles(): jnp.dot(row_pick, x_full, preferred_element_type=jnp.float32)  20 us
  transfers between devices with their start and end apart: 4, of which 3 were waited for; matrix products, arithmetic and copies ran while one was open for 3% of the time, Pallas kernels for 0%

commit v1 on v0

--- a/solution.py
+++ b/solution.py
@@ -4,6 +4,11 @@
 from jax.sharding import PartitionSpec as P
 
 GMAX = 16
+
+
+def gather_over(value, axis, dim):
+    outgoing = jnp.stack([value] * lax.axis_size(axis))
+    return jnp.concatenate(lax.all_to_all(outgoing, axis, 0, 0), axis=dim)
 
 
 def sent_together(arrays, axis, split_dim, concat_dim, along):
@@ -114,7 +119,7 @@
     )
     x_full, z_full, all_basis, rows_all, mask_all = (
         *side_by_side((x_blocks, zinv_blocks), "col", 1, 0),
-        lax.all_gather(near_basis, "col", axis=1, tiled=True),
+        gather_over(near_basis, "col", 1),
         lax.all_gather(near_rows, "col", axis=1, tiled=True),
         lax.all_gather(near_mask, "col", axis=1, tiled=True),
     )

time: 413 us -> 561 us (1.36); the launches traced: 411 us -> 550 us
  blocking collectives: 37.9 us -> 225 us
  waiting for transfers between devices: 87.1 us -> 16.1 us
  matrix products: 126 us -> 136 us
  starting transfers between devices: 9.97 us -> 17.9 us
    all_gather x1, blocking collectives: 21.8 us -> 210 us  [body(): lax.all_gather(near_rows, 'col', axis=1, tiled=True)]
    all_gather x1 -> x0, waiting for transfers between devices: 71 us -> none  [body(): lax.all_gather(near_basis, 'col', axis=1, tiled=True)]
    dot_general x12, matrix products: 8.84 us -> 19.7 us  [pair_tiles(): jnp.dot(row_pick, z_full, preferred_element_type=jnp.float32)]
    all_to_all x0 -> x1, starting transfers between devices: none -> 7.94 us  [gather_over(): return jnp.concatenate(lax.all_to_all(outgoing, axis, 0, 0), axis=dim)]
  transfers between devices with their start and end apart: 4 -> 4, of which waited for: 3 -> 2; matrix products, arithmetic and copies ran while one was open for 3% -> 2% of each run, Pallas kernels for 0% -> 0%
where the time goes in v1:
time: 561 us; the launch traced here: 550 us
  blocking collectives  225 us (40%)
  matrix products  136 us (24%)
  other arithmetic  75.3 us (13%)
  local copies, waits for them, and re-layouts  58.4 us (10%)
  starting transfers between devices  17.9 us (3%)
  waiting for transfers between devices  16.1 us (3%)
  between operations  13.5 us (2%)
  loops' own time  8.38 us (1%)
    all_gather x1, blocking collectives, body(): lax.all_gather(near_rows, 'col', axis=1, tiled=True)  210 us
    mul x12, other arithmetic, pair_tiles(): tile_sum = tile_sum * row_mask[:, None, None] * column_mask[None, None, :]  52.3 us
    dot_general x12, matrix products, pair_tiles(): jnp.einsum('pcn,snk->pcsk', images, near_basis, preferred_element_type=jn...  42.9 us
    dot_general x12, matrix products, pair_tiles(): jnp.einsum('pcn,nk->pck', images, column_pick, preferred_element_type=jnp...  32.8 us
    squeeze x12, local copies, waits for them, and re-layouts, body(): lax.map(pair_tiles, (stacked, x_full, z_full, rows_all, mask_all, near_ba...  20.8 us
    another operation x1, other arithmetic, body(): stacked = jnp.stack([all_x, all_z], axis=2)  20.6 us
    dot_general x12, matrix products, pair_tiles(): jnp.dot(row_pick, x_full, preferred_element_type=jnp.float32)  20 us
    dot_general x12, matrix products, pair_tiles(): jnp.dot(row_pick, z_full, preferred_element_type=jnp.float32)  19.7 us
  transfers between devices with their start and end apart: 4, of which 2 were waited for; matrix products, arithmetic and copies ran while one was open for 2% of the time, Pallas kernels for 0%

profile of v1, /device:TPU:1, one launch (start us, length us, event | category | flops | bytes accessed | tf_op | source)
XLA Modules:
  0.0 550.0 jit_solution(15259061172466822604)
XLA Ops:
  9.1 5.8 %all-to-all-start = ((s32[8,2,129]{2,1,0:T(2,128)}), s32[8,2,129]{2,1,0:T(2,128)S(1)}, u32[]{:S(2)}, u32[]{:S(2)}) async-start(s32[8,2,129]{2,1,0:T(2,128)} %pad_add_fusion), calls=%async_computation | async-start | bytes 32768 | tf_op jit(solution)/shard_map/all_to_all | solution.py:18
  19.5 4.2 all-to-all-start.1
  23.8 14.8 %all-to-all-done.1 = bf16[16,256,128]{2,1,0:T(8,128)(2,1)S(1)} async-done(((bf16[16,256,128]{2,1,0:T(8,128)(2,1)}), bf16[16,256,128]{2,1,0:T(8,128)(2,1)S(1)}, u32[]{:S(2)}, u32[]{:S(2)}) %all-to-all-start.1) | async-done | bytes 1048608 | tf_op jit(solution)/shard_map/all_to_all | solution.py:106
  41.2 6.1 %stack.12 = bf16[16,12,1,256,128]{3,4,1,2,0:T(8,128)(2,1)} broadcast(bf16[12,256,128]{1,2,0:T(8,128)(2,1)S(1)} %copy.33), dimensions={1,3,4} | broadcast | bytes 13369344 | tf_op jit(solution)/shard_map/stack | solution.py:10
  47.3 7.9 %all-to-all-start.2 = ((bf16[16,12,1,256,128]{3,4,1,2,0:T(8,128)(2,1)}), bf16[16,12,1,256,128]{3,4,1,2,0:T(8,128)(2,1)}, u32[]{:S(2)}, u32[]{:S(2)}) async-start(bf16[16,12,1,256,128]{3,4,1,2,0:T(8,128)(2,1)} %stack.12), calls=%async_computation.2 | async-start | bytes 25165824 | tf_op jit(solution)/shard_map/all_to_all | solution.py:11
  56.2 209.8 %all-gather = s32[12,2048]{1,0:T(8,128)S(1)} all-gather(s32[12,128]{1,0:T(8,128)S(1)} %fusion.42), channel_id=2, replica_groups=mesh['row'=8,'col'=16] {'col'}, dimensions={1}, use_global_device_ids=true | all-gather | bytes 104448 | tf_op jit(solution)/shard_map/all_gather | solution.py:123
  266.1 14.8 %all-gather.1 = bf16[16,1,12]{2,1,0:T(2,128)(2,1)S(1)} all-gather(bf16[1,1,12]{2,1,0:T(2,128)(2,1)S(1)} %bitcast.147), channel_id=1, replica_groups=mesh['row'=8,'col'=16] {'col'}, dimensions={0}, use_global_device_ids=true | all-gather | bytes 408 | tf_op jit(solution)/shard_map/all_gather | solution.py:124
  281.0 4.0 fusion.61
  284.9 9.2 %convert_bitcast_fusion = bf16[12,16,1,128,256]{4,3,1,0,2:T(8,128)(2,1)} fusion(bf16[16,12,1,256,128]{3,4,1,2,0:T(8,128)(2,1)} %all-to-all-done.2, bf16[24,256,256]{2,1,0:T(8,128)(2,1)S(1)} %copy-done.2), kind=kOutput, calls=%fused_computation.49 | convolution fusion | flops 3227516928 | bytes 26738688 | tf_op jit(solution)/shard_map/jpnc,jnm->jpcm/dot_general | solution.py:129
  294.1 9.1 %convert_bitcast_fusion.1 = bf16[12,16,1,128,256]{4,3,1,0,2:T(8,128)(2,1)} fusion(bf16[16,12,1,256,128]{3,4,1,2,0:T(8,128)(2,1)} %all-to-all-done.2, bf16[24,256,256]{2,1,0:T(8,128)(2,1)S(1)} %copy-done.2), kind=kOutput, calls=%fused_computation.50 | convolution fusion | flops 3227516928 | bytes 26738688 | tf_op jit(solution)/shard_map/jpnc,jnm->jpcm/dot_general | solution.py:126
  303.2 20.6 %pad_maximum_fusion.3 = bf16[12,16,2,128,256]{4,3,1,0,2:T(8,128)(2,1)} fusion(bf16[12,16,1,128,256]{4,3,1,0,2:T(8,128)(2,1)} %convert_bitcast_fusion, bf16[12,16,1,128,256]{4,3,1,0,2:T(8,128)(2,1)} %convert_bitcast_fusion.1), kind=kLoop, calls=%fused_computation.44 | loop fusion | flops 12582912 | bytes 50331648 | tf_op jit(solution)/shard_map/stack | solution.py:132
  323.7 218.7 %while.10 = (s32[]{:T(128)}, f32[12,2048,128]{2,1,0:T(8,128)}, bf16[12,16,2,128,256]{4,3,1,0,2:T(8,128)(2,1)}, s32[12,16,128]{2,1,0:T(8,128)S(1)}, bf16[12,256,2...) while((s32[]{:T(128)}, f32[12,2048,128]{2,1,0:T(8,128)}, ...), condition=%wide.region_3.4_spmd, body=%wide.region_2.3_spmd.sunk | while | flops 1648656384 | bytes 39161648 | solution.py:133
  331.7 3.6 fusion.77
  336.6 4.4 fusion.81
  349.9 3.6 fusion.77
  354.8 4.4 fusion.81
  368.2 3.6 fusion.77
  373.0 4.4 fusion.81
  386.4 3.6 fusion.77
  391.2 4.4 fusion.81
  404.6 3.6 fusion.77
  409.5 4.4 fusion.81
  422.8 3.6 fusion.77
  427.7 4.4 fusion.81
  441.1 3.6 fusion.77
  445.9 4.4 fusion.81
  464.1 4.4 fusion.81
  482.4 4.4 fusion.81
  500.6 4.4 fusion.81
  514.0 3.6 fusion.77
  518.8 4.4 fusion.81
  537.0 4.4 fusion.81
  (165 shorter events, 141.1 us)
Async XLA Ops:
  6.5 1.8 copy-start
  9.1 10.4 %all-to-all-start = ((s32[8,2,129]{2,1,0:T(2,128)}), s32[8,2,129]{2,1,0:T(2,128)S(1)}, u32[]{:S(2)}, u32[]{:S(2)}) async-start(s32[8,2,129]{2,1,0:T(2,128)} %pad_add_fusion), calls=%async_computation | async-start | bytes 32768 | tf_op jit(solution)/shard_map/all_to_all | solution.py:18
  19.5 19.2 %all-to-all-start.1 = ((bf16[16,256,128]{2,1,0:T(8,128)(2,1)}), bf16[16,256,128]{2,1,0:T(8,128)(2,1)S(1)}, u32[]{:S(2)}, u32[]{:S(2)}) async-start(bf16[16,256,128]{2,1,0:T(8,128)(2,1)} %bitcast.48), calls=%async_computation.1 | async-start | bytes 2097152 | tf_op jit(solution)/shard_map/all_to_all | solution.py:106
  47.3 8.0 %copy-start.3 = (bf16[12,16,256]{2,1,0:T(8,128)(2,1)S(1)}, bf16[12,16,256]{2,1,0:T(8,128)(2,1)}, u32[]{:S(2)}) copy-start(bf16[12,16,256]{2,1,0:T(8,128)(2,1)} %param.11) | copy-start | bytes 294916
  47.3 8.0 %copy-start.4 = (bf16[12,16,256]{2,1,0:T(8,128)(2,1)S(1)}, bf16[12,16,256]{2,1,0:T(8,128)(2,1)}, u32[]{:S(2)}) copy-start(bf16[12,16,256]{2,1,0:T(8,128)(2,1)} %param.10) | copy-start | bytes 294916
  47.3 237.6 %all-to-all-start.2 = ((bf16[16,12,1,256,128]{3,4,1,2,0:T(8,128)(2,1)}), bf16[16,12,1,256,128]{3,4,1,2,0:T(8,128)(2,1)}, u32[]{:S(2)}, u32[]{:S(2)}) async-start(bf16[16,12,1,256,128]{3,4,1,2,0:T(8,128)(2,1)} %stack.12), calls=%async_computation.2 | async-start | bytes 25165824 | tf_op jit(solution)/shard_map/all_to_all | solution.py:11
  55.2 225.7 %all-gather.4.cloned.1.call-start = ((), (), s32[]{:S(2)}) async-start(), calls=%async_computation.3 | async-start | bytes 3342336 | tf_op jit(solution)/shard_map/all_gather | solution.py:32
  281.0 4.0 copy-start.2
  542.4 0.7 copy-start.1
Sparse Core Ops, SparseCore 0:
  58.2 198.3 all-gather.3
